TPU v7x, 1024 devices: a whole 8x8x8 slice. The times are simulated.
1024 devices in a mesh: ctx: 64 (over y, x), tp: 8 (over z), grp: 2 (over core).
Axes of the slice: x: 8, y: 8, z: 8, core: 2. Of those that a mesh axis runs over, the one named last changes fastest.
Arguments:
- patches: bfloat16 [8192, 5120], P('ctx'), may hold values from -6 to 6
- route_count: int32 [64, 64], replicated, may hold values from 0 to 2, as said below
- text_states: bfloat16 [8192, 4096], P('ctx', ('tp', 'grp')), may hold values from -6 to 6
- segment_ids: int32 [8192], replicated, may hold values from 0 to 3, never falling along the last dimension, each value on 1 to 4096 neighbouring positions
- vision_gain: float32 [1280], replicated, may hold values from 0.1 to 1.9
- merge_up: bfloat16 [5120, 2560], P(None, ('tp', 'grp')), may hold values from -0.078125 to 0.078125
- merge_down: bfloat16 [2560, 4096], P(('tp', 'grp')), may hold values from -0.125 to 0.125
- norm_gain: float32 [4096], replicated, may hold values from 0.1 to 1.9
- query_weight: bfloat16 [4096, 4096], P(None, ('tp', 'grp')), may hold values from -0.62928387 to 0.62928387
- kv_weight: bfloat16 [4096, 2048], P(None, 'tp'), may hold values from -0.4578688 to 0.4578688
Outputs:
- attended: bfloat16 [8192, 4096], P('ctx', ('tp', 'grp'))
Inputs may be any that keep to these rules, and one draw needn't show every extreme that they name: route_count[c, d] counts the live rows among the 2 rows that source c holds for owner d; at least one owner gets 2 live rows from every source. `segment_ids`: never falling along the packed batch; a segment has at most 4096 positions.
All inputs are finite; a program needn't handle non-finite values.
Results may differ from a plain program's by a relative error of at most 0.04.
Values may be sent and summed in bfloat16 or wider, within the bound.
No kernel may reach another device: no remote copies, remote signals or barrier semaphores. Data moves between devices by JAX's collectives and lax.ppermute only.
A program may use at most 64 MiB of HBM per device.

v0:
```python
import functools

import jax
import jax.numpy as jnp
from jax import lax
from jax.experimental import pallas as pl
from jax.experimental.pallas import tpu as pltpu
from jax.sharding import Mesh
from jax.sharding import PartitionSpec as P

HD = 128
CTX = ("ctx_0", "ctx_q", "ctx_p")
EPSILON = 1e-06
NEGATIVE = -1e30
LOG2E = 1.4426950408889634
F32 = jnp.float32
BF16 = jnp.bfloat16
VMEM = pl.BlockSpec(memory_space=pltpu.VMEM)
SMEM = pl.BlockSpec(memory_space=pltpu.SMEM)


def params(*semantics):
    return pltpu.CompilerParams(
        dimension_semantics=semantics or None, vmem_limit_bytes=40 << 20
    )


def exchange(parts, axis):
    return lax.all_to_all(parts, axis, split_axis=0, concat_axis=0, tiled=True)


def up_kernel(x_hbm, gain_hbm, w_hbm, out_ref, x_ref, gain_ref, w_ref, sems, gain_sem):
    groups, rows, vis = x_ref.shape
    gain_copy = pltpu.make_async_copy(gain_hbm, gain_ref, gain_sem)
    gain_copy.start()
    copies = []
    for k in range(groups):
        cols = pl.ds(k * vis, vis)
        both = (
            pltpu.make_async_copy(x_hbm.at[:, cols], x_ref.at[k], sems.at[0, k]),
            pltpu.make_async_copy(w_hbm.at[:, cols], w_ref.at[k], sems.at[1, k]),
        )
        for copy in both:
            copy.start()
        copies.append(both)
    gain_copy.wait()
    gain = gain_ref[...].reshape(1, vis)
    total = jnp.zeros((rows, w_ref.shape[1]), F32)
    for k in range(groups):
        for copy in copies[k]:
            copy.wait()
        x = x_ref[k].astype(F32)
        scale = lax.rsqrt(jnp.mean(x * x, axis=-1, keepdims=True) + EPSILON)
        normed = (x * scale * gain).astype(BF16)
        total += lax.dot_general(
            normed, w_ref[k], (((1,), (1,)), ((), ())), preferred_element_type=F32
        )
    hidden = 0.5 * total * (1.0 + lax.erf(total * 0.5**0.5))
    out_ref[...] = hidden.astype(BF16).reshape(out_ref.shape)


def merge_up_rows(patches, vision_gain, merge_up, blocks):
    rows, width = patches.shape
    vis = vision_gain.shape[0]
    units = merge_up.shape[1]
    groups = width // vis
    return pl.pallas_call(
        up_kernel,
        in_specs=[pl.BlockSpec(memory_space=pltpu.HBM)] * 3,
        out_specs=VMEM,
        out_shape=jax.ShapeDtypeStruct((blocks, rows // blocks, units), BF16),
        scratch_shapes=[
            pltpu.VMEM((groups, rows, vis), BF16),
            pltpu.VMEM((vis,), F32),
            pltpu.VMEM((groups, units, vis), BF16),
            pltpu.SemaphoreType.DMA((2, groups)),
            pltpu.SemaphoreType.DMA,
        ],
        compiler_params=params(),
        name="merge_up",
    )(patches, vision_gain, merge_up.T)


def shuffle_kernel(n_x, rows_ref, out_ref):
    n_y, inner, units = rows_ref.shape
    total, bucket = n_y * inner, inner // n_x
    target = lax.broadcasted_iota(jnp.int32, (total, total), 0)
    row = lax.broadcasted_iota(jnp.int32, (total, total), 1)
    to_x, rest = target // (n_y * bucket), target % (n_y * bucket)
    wanted = (rest // bucket) * inner + to_x * bucket + rest % bucket
    select = jnp.where(row == wanted, 1.0, 0.0).astype(BF16)
    rows = rows_ref[...].reshape(total, units)
    out = jnp.dot(select, rows, preferred_element_type=F32).astype(BF16)
    out_ref[...] = out.reshape(out_ref.shape)


def shuffle_rows(rows, n_x):
    n_y, inner, units = rows.shape
    return pl.pallas_call(
        functools.partial(shuffle_kernel, n_x),
        in_specs=[VMEM],
        out_specs=VMEM,
        out_shape=jax.ShapeDtypeStruct((n_x, n_y * inner // n_x, units), BF16),
        compiler_params=params(),
        name="shuffle",
    )(rows)


def owner_column(owner, route):
    lanes = lax.broadcasted_iota(jnp.int32, route.shape, 1)
    return jnp.sum(jnp.where(lanes == owner, route, 0), axis=1, keepdims=True)


def down_kernel(n_y, n_x, owner_ref, route_ref, arrived_ref, w_ref, out_ref):
    grp, tp, rows, width = out_ref.shape
    sources = route_ref.shape[0]
    bucket = rows // sources
    column = owner_column(owner_ref[0], route_ref[...])
    source = lax.broadcasted_iota(jnp.int32, (sources, rows), 0)
    row = lax.broadcasted_iota(jnp.int32, (sources, rows), 1)
    sender = (row // bucket % n_y) * n_x + row // (bucket * n_y)
    before = jnp.sum(jnp.where(source < sender, column, 0), axis=0, keepdims=True)
    count = jnp.sum(jnp.where(source == sender, column, 0), axis=0, keepdims=True)
    place = lax.rem(lax.broadcasted_iota(jnp.int32, (1, rows), 1), bucket)
    target = jnp.where(place < count, before + place, -1)
    slot = lax.broadcasted_iota(jnp.int32, (rows, rows), 0)
    select = jnp.where(slot == target, 1.0, 0.0).astype(BF16)
    picked = jnp.dot(select, arrived_ref[...], preferred_element_type=F32).astype(BF16)
    for t in range(tp):
        for g in range(grp):
            lo = (t * grp + g) * width
            out_ref[g, t] = jnp.dot(
                picked, w_ref[:, lo : lo + width], preferred_element_type=F32
            ).astype(BF16)


def merge_down_rows(owner, route_count, arrived, merge_down, n_y, n_x, tp, grp):
    width = merge_down.shape[1] // (tp * grp)
    return pl.pallas_call(
        functools.partial(down_kernel, n_y, n_x),
        in_specs=[SMEM, VMEM, VMEM, VMEM],
        out_specs=VMEM,
        out_shape=jax.ShapeDtypeStruct((grp, tp, arrived.shape[0], width), BF16),
        compiler_params=params(),
        name="merge_down",
    )(owner, route_count, arrived, merge_down)


def pair_kernel(parts_ref, out_ref):
    out_ref[...] = (parts_ref[0].astype(F32) + parts_ref[1].astype(F32)).astype(BF16)


def pair_sum(parts):
    return pl.pallas_call(
        pair_kernel,
        in_specs=[VMEM],
        out_specs=VMEM,
        out_shape=jax.ShapeDtypeStruct(parts.shape[1:], BF16),
        compiler_params=params(),
        name="pair_sum",
    )(parts)


def place_kernel(owner_ref, route_ref, parts_ref, text_ref, out_ref):
    total = parts_ref[0].astype(F32)
    for k in range(1, parts_ref.shape[0]):
        total += parts_ref[k].astype(F32)
    visual = jnp.sum(owner_column(owner_ref[0], route_ref[...]), axis=0, keepdims=True)
    slot = lax.broadcasted_iota(jnp.int32, total.shape, 0)
    placed = jnp.where(slot < visual, total, text_ref[...].astype(F32)).astype(BF16)
    for k in range(out_ref.shape[0]):
        out_ref[k] = placed


def place_rows(owner, route_count, parts, text_states):
    return pl.pallas_call(
        place_kernel,
        in_specs=[SMEM, VMEM, VMEM, VMEM],
        out_specs=VMEM,
        out_shape=jax.ShapeDtypeStruct(parts.shape, BF16),
        compiler_params=params(),
        name="place",
    )(owner, route_count, parts, text_states)


def project_kernel(half_ref, parts_ref, gain_ref, wq_ref, wkv_ref, q_ref, kv_ref):
    grp, tp, rows, width = parts_ref.shape
    squares = jnp.zeros((rows, width), F32)
    for g in range(grp):
        for t in range(tp):
            x = parts_ref[g, t].astype(F32)
            squares += x * x
    mean = jnp.sum(squares, axis=-1, keepdims=True) / (grp * tp * width)
    scale = lax.rsqrt(mean + EPSILON)
    q = jnp.zeros((rows, wq_ref.shape[1]), F32)
    kv = jnp.zeros((rows, wkv_ref.shape[1]), F32)
    for t in range(tp):
        for g in range(grp):
            lo = (t * grp + g) * width
            gain = gain_ref[lo : lo + width].reshape(1, width)
            normal = (parts_ref[g, t].astype(F32) * scale * gain).astype(BF16)
            q += jnp.dot(normal, wq_ref[lo : lo + width, :], preferred_element_type=F32)
            kv += jnp.dot(normal, wkv_ref[lo : lo + width, :], preferred_element_type=F32)
    q = q.astype(BF16)
    for k in range(q_ref.shape[0]):
        q_ref[k] = q
    part = kv_ref.shape[1]
    own = kv[:part]
    for g in range(1, rows // part):
        own = jnp.where(half_ref[0] == g, kv[g * part : (g + 1) * part], own)
    for k in range(kv_ref.shape[0]):
        kv_ref[k] = own.astype(BF16)


def project(half, parts, norm_gain, query_weight, kv_weight, q_copies, kv_copies):
    grp, _, rows, _ = parts.shape
    return pl.pallas_call(
        project_kernel,
        in_specs=[SMEM] + [VMEM] * 4,
        out_specs=[VMEM] * 2,
        out_shape=[
            jax.ShapeDtypeStruct((q_copies, rows, query_weight.shape[1]), BF16),
            jax.ShapeDtypeStruct((kv_copies, rows // grp, kv_weight.shape[1]), BF16),
        ],
        compiler_params=params(),
        name="project",
    )(half, parts, norm_gain, query_weight, kv_weight)


def seen_kernel(route_ref, seen_ref):
    blocks, rows = seen_ref.shape
    visual = jnp.sum(route_ref[...].T, axis=1, keepdims=True)
    block = lax.broadcasted_iota(jnp.int32, (blocks, rows), 0)
    lane = lax.broadcasted_iota(jnp.int32, (blocks, rows), 1)
    seen_ref[...] = jnp.where(lane < visual, -1, block * rows + lane)


def seen_from(route_count, rows):
    return pl.pallas_call(
        seen_kernel,
        in_specs=[VMEM],
        out_specs=VMEM,
        out_shape=jax.ShapeDtypeStruct((route_count.shape[1], rows), jnp.int32),
        compiler_params=params(),
        name="seen",
    )(route_count)


def attend_kernel(pair, home_ref, ends_ref, q_ref, kv_ref, seg_ref, seen_ref, out_ref):
    _, rows, q_width = q_ref.shape
    heads = q_width // HD
    block = pl.program_id(0)
    pairs = kv_ref.shape[1] // pair
    n_x = pl.num_programs(0) * pair
    q_block = home_ref[0] * n_x + block * pair + home_ref[2]
    column = home_ref[1] * pair
    first = jnp.minimum(
        (jnp.maximum(ends_ref[0, block] - column - (pair - 1), 0) + n_x - 1) // n_x,
        pairs - 1,
    )
    last = (ends_ref[1, block] - column + n_x) // n_x - 1
    near = min(5, pairs)

    def rows_of(index, cols):
        return jnp.concatenate(
            [kv_ref[:, index * pair + w, :, cols].reshape(rows, HD) for w in range(pair)], axis=0
        )

    def attend_to(start, count):
        q_seg = jnp.broadcast_to(seg_ref[pl.ds(q_block, 1), :], (rows, rows)).T
        q_seg = jnp.concatenate([q_seg] * pair, axis=1)
        q_pos = q_block * rows + lax.broadcasted_iota(jnp.int32, (rows, pair * rows), 0)
        q = jnp.concatenate([q_ref[0, :, h * HD : (h + 1) * HD] for h in range(heads)], axis=0)
        scores = []
        top = None
        for k in range(count):
            keys = rows_of(start + k, slice(0, HD))
            wanted = [(start + k) * n_x + column + w for w in range(pair)]
            k_seg = jnp.concatenate([seg_ref[pl.ds(w, 1), :] for w in wanted], axis=1)
            seen = jnp.concatenate([seen_ref[pl.ds(w, 1), :] for w in wanted], axis=1)
            allowed = (q_seg == k_seg) & (seen <= q_pos)
            s = lax.dot_general(
                q, keys, (((1,), (1,)), ((), ())), preferred_element_type=F32
            ) * (HD**-0.5 * LOG2E)
            s = jnp.concatenate(
                [jnp.where(allowed, s[h * rows : (h + 1) * rows], NEGATIVE) for h in range(heads)],
                axis=0,
            )
            scores.append(s)
            top = s if top is None else jnp.maximum(top, s)
        top = jnp.max(top, axis=1, keepdims=True)
        floor = jnp.maximum(top, 0.5 * NEGATIVE)
        total = jnp.zeros((heads * rows, pair * rows), F32)
        mixed = jnp.zeros((heads * rows, HD), F32)
        for k in range(count):
            weights = jnp.exp2(scores[k] - floor)
            total += weights
            values = rows_of(start + k, slice(HD, 2 * HD))
            mixed += jnp.dot(weights.astype(BF16), values, preferred_element_type=F32)
        total = jnp.sum(total, axis=1, keepdims=True)
        empty = total == 0.0
        mixed = mixed / jnp.where(empty, 1.0, total)
        mass = jnp.where(empty, NEGATIVE, floor + jnp.log2(jnp.where(empty, 1.0, total)))
        for h in range(heads):
            cols = slice(h * HD, (h + 1) * HD)
            part = slice(h * rows, (h + 1) * rows)
            out_ref[0, :rows, cols] = mixed[part].astype(BF16)
            flat = jnp.broadcast_to(mass[part], (rows, rows)).T[:16]
            high = flat.astype(BF16).astype(F32)
            second = lax.broadcasted_iota(jnp.int32, flat.shape, 0) >= 8
            out_ref[0, rows:, cols] = jnp.where(second, flat - high, high).astype(BF16)

    close = last - first < near
    if near == pairs:
        attend_to(0, pairs)
    else:
        pl.when(close)(lambda: attend_to(jnp.minimum(first, pairs - near), near))
        pl.when(jnp.logical_not(close))(lambda: attend_to(0, pairs))


def attend(pair, home, ends, q_parts, kv_parts, segment_rows, seen):
    q_blocks, rows, width = q_parts.shape
    return pl.pallas_call(
        functools.partial(attend_kernel, pair),
        grid=(q_blocks,),
        in_specs=[
            SMEM,
            SMEM,
            pl.BlockSpec((1, rows, width), lambda k: (k, 0, 0)),
            VMEM,
            VMEM,
            VMEM,
        ],
        out_specs=pl.BlockSpec((1, rows + 16, width), lambda k: (k, 0, 0)),
        out_shape=jax.ShapeDtypeStruct((q_blocks, rows + 16, width), BF16),
        compiler_params=params("arbitrary"),
        name="attend",
    )(home, ends, q_parts, kv_parts, segment_rows, seen)


def combine_kernel(parts_ref, out_ref):
    count = parts_ref.shape[0]
    rows, width = out_ref.shape
    for h in range(width // HD):
        cols = slice(h * HD, (h + 1) * HD)
        masses = []
        for k in range(count):
            stats = parts_ref[k, rows:, cols].astype(F32)
            flat = stats[0:1] + stats[8:9]
            masses.append(jnp.broadcast_to(flat, (rows, HD)).T)
        top = functools.reduce(jnp.maximum, masses)
        total = jnp.zeros((rows, HD), F32)
        mixed = jnp.zeros((rows, HD), F32)
        for k in range(count):
            weight = jnp.exp2(masses[k] - top)
            total += weight
            mixed += weight * parts_ref[k, :rows, cols].astype(F32)
        out_ref[:, cols] = (mixed / total).astype(BF16)


def combine(parts):
    return pl.pallas_call(
        combine_kernel,
        in_specs=[VMEM],
        out_specs=VMEM,
        out_shape=jax.ShapeDtypeStruct((parts.shape[1] - 16, parts.shape[2]), BF16),
        compiler_params=params(),
        name="combine",
    )(parts)


def block_ends(own_rows, segment_ids, rows):
    first, last = own_rows[:, 0], own_rows[:, -1]
    below = jnp.sum((segment_ids[None] < first[:, None]).astype(jnp.int32), axis=1)
    upto = jnp.sum((segment_ids[None] <= last[:, None]).astype(jnp.int32), axis=1)
    return jnp.stack([below // rows, (upto - 1) // rows])


def shards(
    patches,
    route_count,
    text_states,
    segment_ids,
    vision_gain,
    merge_up,
    merge_down,
    norm_gain,
    query_weight,
    kv_weight,
):
    tp, grp = lax.axis_size("tp"), lax.axis_size("grp")
    n_y, n_q, pair = lax.axis_size("ctx_0"), lax.axis_size("ctx_q"), lax.axis_size("ctx_p")
    y, q_at, p_at = lax.axis_index("ctx_0"), lax.axis_index("ctx_q"), lax.axis_index("ctx_p")
    n_x, x = n_q * pair, q_at * pair + p_at
    rows = patches.shape[0]
    home = jnp.stack([y, q_at, p_at]).astype(jnp.int32)
    half = lax.axis_index("grp").astype(jnp.int32).reshape(1)
    owner = (y * n_x + x).astype(jnp.int32).reshape(1)
    segment_rows = segment_ids.reshape(-1, rows)
    own_rows = lax.dynamic_slice(
        segment_ids.reshape(n_y, n_q, pair, rows), (y, 0, p_at, 0), (1, n_q, 1, rows)
    )
    ends = block_ends(own_rows.reshape(n_q, rows), segment_ids, rows)
    seen = seen_from(route_count, rows)

    hidden = merge_up_rows(patches, vision_gain, merge_up, n_y)
    hidden = exchange(shuffle_rows(exchange(hidden, "ctx_0"), n_x), CTX[1:])
    partial_sums = merge_down_rows(
        owner, route_count, hidden.reshape(rows, -1), merge_down, n_y, n_x, tp, grp
    )
    partial_sums = pair_sum(exchange(partial_sums, "grp"))
    partial_sums = exchange(partial_sums, "tp")
    placed = place_rows(owner, route_count, partial_sums, text_states)
    packed = exchange(placed, "tp")
    packed = exchange(jnp.broadcast_to(packed[None], (grp, *packed.shape)), "grp")
    packed = packed.reshape(grp, tp, rows, -1)
    q, kv = project(half, packed, norm_gain, query_weight, kv_weight, n_q, n_y * pair)
    kv = exchange(kv, ("ctx_0", "ctx_p"))
    kv = exchange(jnp.broadcast_to(kv[None], (grp, *kv.shape)), "grp")
    q = exchange(q, "ctx_q")
    parts = attend(pair, home, ends, q, kv, segment_rows, seen)
    return combine(exchange(parts, "ctx_q"))


def solution(mesh):
    finer = Mesh(
        mesh.devices.reshape(8, 4, 2, mesh.shape["tp"], mesh.shape["grp"]),
        (*CTX, "tp", "grp"),
    )
    ctx = CTX
    return jax.shard_map(
        shards,
        mesh=finer,
        in_specs=(
            P(ctx, None),
            P(),
            P(ctx, ("tp", "grp")),
            P(),
            P(),
            P(None, ("tp", "grp")),
            P(("tp", "grp"), None),
            P(),
            P(None, ("tp", "grp")),
            P(None, "tp"),
        ),
        out_specs=P(ctx, ("tp", "grp")),
        check_vma=False,
    )
```

profile of v0, /device:TPU:1, one launch (start us, length us, event | category | flops | bytes accessed | tf_op | source)
XLA Modules:
  0.0 163.5 jit_solution(18027592714271687466)
XLA Ops:
  0.0 1.4 copy-done.2
  1.4 1.3 copy-done.3
  2.8 0.7 copy-done.9
  3.5 1.9 %merge_up.1 = bf16[8,16,160]{2,1,0:T(8,128)(2,1)S(1)} custom-call(bf16[128,5120]{1,0:T(8,128)(2,1)S(1)} %copy-done.3, f32[1280]{0:T(1024)S(1)} %copy-done.9, bf16[160,5120]{1,0:T(8,128)(2,1)S(1)} %bitcast.26), custom_call_target="tpu_custom_call" | custom-call | tf_op jit(solution)/shard_map/merge_up/pallas_call | solution.py:67
  5.4 15.1 %all_to_all.50.rows_ref = bf16[8,16,160]{2,1,0:T(8,128)(2,1)S(1)} all-to-all(bf16[8,16,160]{2,1,0:T(8,128)(2,1)S(1)} %merge_up.1), channel_id=1, replica_groups=mesh['ctx_0'=8,'ctx_q'=4,'ctx_p'=2,'tp'=8,'grp'=2] {'ctx_0'}, dimensions={0} | all-to-all | bytes 81920 | tf_op jit(solution)/shard_map/all_to_all | solution.py:29
  20.5 0.8 shuffle.1
  21.3 6.5 %all-to-all-start.1 = ((bf16[8,16,160]{2,1,0:T(8,128)(2,1)}), bf16[8,16,160]{2,1,0:T(8,128)(2,1)S(1)}, u32[]{:S(2)}, u32[]{:S(2)}) async-start(bf16[8,16,160]{2,1,0:T(8,128)(2,1)} %shuffle.1), calls=%async_computation.1 | async-start | bytes 131072 | tf_op jit(solution)/shard_map/all_to_all | solution.py:29
  27.8 7.2 %all-to-all-done.1 = bf16[8,16,160]{2,1,0:T(8,128)(2,1)S(1)} async-done(((bf16[8,16,160]{2,1,0:T(8,128)(2,1)}), bf16[8,16,160]{2,1,0:T(8,128)(2,1)S(1)}, u32[]{:S(2)}, u32[]{:S(2)}) %all-to-all-start.1) | async-done | bytes 40992 | tf_op jit(solution)/shard_map/all_to_all | solution.py:29
  35.0 0.6 merge_down.1
  35.7 11.9 %all_to_all.51.parts_ref = bf16[2,8,128,256]{3,2,1,0:T(8,128)(2,1)S(1)} all-to-all(bf16[2,8,128,256]{3,2,1,0:T(8,128)(2,1)S(1)} %merge_down.1), channel_id=1, replica_groups=mesh['ctx_0'=8,'ctx_q'=4,'ctx_p'=2,'tp'=8,'grp'=2] {'grp'}, dimensions={0} | all-to-all | bytes 2097152 | tf_op jit(solution)/shard_map/all_to_all | solution.py:29
  47.5 0.1 pair_sum.1
  47.7 28.8 %all_to_all.52.parts_ref = bf16[8,128,256]{2,1,0:T(8,128)(2,1)S(1)} all-to-all(bf16[8,128,256]{2,1,0:T(8,128)(2,1)S(1)} %pair_sum.1), channel_id=1, replica_groups=mesh['ctx_0'=8,'ctx_q'=4,'ctx_p'=2,'tp'=8,'grp'=2] {'tp'}, dimensions={0} | all-to-all | bytes 1048576 | tf_op jit(solution)/shard_map/all_to_all | solution.py:29
  76.4 1.0 place.1
  77.4 3.5 %all-to-all-start.4 = ((bf16[8,128,256]{2,1,0:T(8,128)(2,1)}), bf16[8,128,256]{2,1,0:T(8,128)(2,1)S(1)}, u32[]{:S(2)}, u32[]{:S(2)}) async-start(bf16[8,128,256]{2,1,0:T(8,128)(2,1)} %place.1), calls=%async_computation.4 | async-start | bytes 1048576 | tf_op jit(solution)/shard_map/all_to_all | solution.py:29
  80.9 0.0 copy-start
  80.9 15.9 %all-to-all-done.4 = bf16[8,128,256]{2,1,0:T(8,128)(2,1)S(1)} async-done(((bf16[8,128,256]{2,1,0:T(8,128)(2,1)}), bf16[8,128,256]{2,1,0:T(8,128)(2,1)S(1)}, u32[]{:S(2)}, u32[]{:S(2)}) %all-to-all-start.4) | async-done | bytes 524320 | tf_op jit(solution)/shard_map/all_to_all | solution.py:29
  96.8 0.1 broadcast_in_dim.4
  96.9 6.6 %all_to_all.53.parts_ref = bf16[2,8,128,256]{3,2,1,0:T(8,128)(2,1)S(1)} all-to-all(bf16[2,8,128,256]{3,2,1,0:T(8,128)(2,1)S(1)} %broadcast_in_dim.4), channel_id=1, replica_groups=mesh['ctx_0'=8,'ctx_q'=4,'ctx_p'=2,'tp'=8,'grp'=2] {'grp'}, dimensions={0} | all-to-all | bytes 2097152 | tf_op jit(solution)/shard_map/all_to_all | solution.py:29
  103.6 1.6 copy-done.1
  105.2 1.9 %project.1 = (bf16[4,128,256]{2,1,0:T(8,128)(2,1)S(1)}, bf16[16,64,256]{2,1,0:T(8,128)(2,1)}) custom-call(s32[1]{0:T(128)} %bitcast.7.half_ref, bf16[2,8,128,256]{3,2,1,0:T(8,128)(2,1)S(1)} %all_to_all.53.parts_ref, f32[4096]{0:T(1024)S(1)} %copy-done.8, bf16[4096,256]{1,0:T(8,128)(2,1)S(1)} %copy-done, bf16[4096,256]{1,0:T(8,128)(2,1)S(1)} %copy-done.1), custom_call_target="tpu_custom_call" | custom-call | tf_op jit(solution)/shard_map/project/pallas_call | solution.py:217
  107.0 12.3 %all_to_all.54.q_ref = bf16[4,128,256]{2,1,0:T(8,128)(2,1)S(1)} all-to-all(bf16[4,128,256]{2,1,0:T(8,128)(2,1)S(1)} %get-tuple-element.7), channel_id=1, replica_groups=mesh['ctx_0'=8,'ctx_q'=4,'ctx_p'=2,'tp'=8,'grp'=2] {'ctx_q'}, dimensions={0} | all-to-all | bytes 524288 | tf_op jit(solution)/shard_map/all_to_all | solution.py:29
  119.4 3.6 %all-to-all-start.7 = ((bf16[16,64,256]{2,1,0:T(8,128)(2,1)}), bf16[16,64,256]{2,1,0:T(8,128)(2,1)S(1)}, u32[]{:S(2)}, u32[]{:S(2)}) async-start(bf16[16,64,256]{2,1,0:T(8,128)(2,1)} %get-tuple-element.8), calls=%async_computation.7 | async-start | bytes 1048576 | tf_op jit(solution)/shard_map/all_to_all | solution.py:29
  122.9 0.2 seen.1.seen_ref
  123.1 0.1 pad_add_fusion.1.home_ref
  123.2 0.2 slice_reduce_fusion.1
  123.4 0.3 convert_reduce_fusion.1
  123.7 14.3 %all-to-all-done.7 = bf16[16,64,256]{2,1,0:T(8,128)(2,1)S(1)} async-done(((bf16[16,64,256]{2,1,0:T(8,128)(2,1)}), bf16[16,64,256]{2,1,0:T(8,128)(2,1)S(1)}, u32[]{:S(2)}, u32[]{:S(2)}) %all-to-all-start.7) | async-done | bytes 524320 | tf_op jit(solution)/shard_map/all_to_all | solution.py:29
  138.0 0.1 broadcast_in_dim.5
  138.1 7.1 %all_to_all.55.kv_ref = bf16[2,16,64,256]{3,2,1,0:T(8,128)(2,1)S(1)} all-to-all(bf16[2,16,64,256]{3,2,1,0:T(8,128)(2,1)S(1)} %broadcast_in_dim.5), channel_id=1, replica_groups=mesh['ctx_0'=8,'ctx_q'=4,'ctx_p'=2,'tp'=8,'grp'=2] {'grp'}, dimensions={0} | all-to-all | bytes 2097152 | tf_op jit(solution)/shard_map/all_to_all | solution.py:29
  145.2 4.3 %attend.1 = bf16[4,144,256]{2,1,0:T(8,128)(2,1)S(1)} custom-call(s32[3]{0:T(128)S(1)} %pad_add_fusion.1.home_ref, s32[2,4]{1,0:T(2,128)S(1)} %pad_add_fusion.ends_ref, bf16[4,128,256]{2,1,0:T(8,128)(2,1)S(1)} %all_to_all.54.q_ref, bf16[2,16,64,256]{3,2,1,0:T(8,128)(2,1)S(1)} %all_to_all.55.kv_ref, s32[64,128]{1,0:T(8,128)S(1)} %bitcast.29, ...), custom_call_target="tpu_custom_call" | custom-call | tf_op jit(solution)/shard_map/attend/pallas_call | solution.py:323
  149.5 13.1 %all_to_all.56.parts_ref = bf16[4,144,256]{2,1,0:T(8,128)(2,1)S(1)} all-to-all(bf16[4,144,256]{2,1,0:T(8,128)(2,1)S(1)} %attend.1), channel_id=1, replica_groups=mesh['ctx_0'=8,'ctx_q'=4,'ctx_p'=2,'tp'=8,'grp'=2] {'ctx_q'}, dimensions={0} | all-to-all | bytes 589824 | tf_op jit(solution)/shard_map/all_to_all | solution.py:29
  162.7 0.9 combine.1
  (18 shorter events, 0.1 us)
Async XLA Ops:
  0.0 1.4 copy-start.2
  1.4 1.3 copy-start.3
  2.7 0.7 copy-start.9
  3.4 31.6 %copy-start.4 = (bf16[160,4096]{1,0:T(8,128)(2,1)S(1)}, bf16[160,4096]{1,0:T(8,128)(2,1)}, u32[]{:S(2)}) copy-start(bf16[160,4096]{1,0:T(8,128)(2,1)} %w_ref.1) | copy-start | bytes 3932164
  3.4 31.6 %copy-start.5 = (s32[64,64]{1,0:T(8,128)S(1)}, s32[64,64]{1,0:T(8,128)}, u32[]{:S(2)}) copy-start(s32[64,64]{1,0:T(8,128)} %route_ref.5) | copy-start | bytes 49156
  21.3 13.7 %all-to-all-start.1 = ((bf16[8,16,160]{2,1,0:T(8,128)(2,1)}), bf16[8,16,160]{2,1,0:T(8,128)(2,1)S(1)}, u32[]{:S(2)}, u32[]{:S(2)}) async-start(bf16[8,16,160]{2,1,0:T(8,128)(2,1)} %shuffle.1), calls=%async_computation.1 | async-start | bytes 131072 | tf_op jit(solution)/shard_map/all_to_all | solution.py:29
  47.5 28.9 %copy-start.7 = (bf16[128,256]{1,0:T(8,128)(2,1)S(1)}, bf16[128,256]{1,0:T(8,128)(2,1)}, u32[]{:S(2)}) copy-start(bf16[128,256]{1,0:T(8,128)(2,1)} %text_ref.1) | copy-start | bytes 196612
  77.4 19.4 %all-to-all-start.4 = ((bf16[8,128,256]{2,1,0:T(8,128)(2,1)}), bf16[8,128,256]{2,1,0:T(8,128)(2,1)S(1)}, u32[]{:S(2)}, u32[]{:S(2)}) async-start(bf16[8,128,256]{2,1,0:T(8,128)(2,1)} %place.1), calls=%async_computation.4 | async-start | bytes 1048576 | tf_op jit(solution)/shard_map/all_to_all | solution.py:29
  80.9 22.7 %copy-start = (bf16[4096,256]{1,0:T(8,128)(2,1)S(1)}, bf16[4096,256]{1,0:T(8,128)(2,1)}, u32[]{:S(2)}) copy-start(bf16[4096,256]{1,0:T(8,128)(2,1)} %wq_ref.1) | copy-start | bytes 6291460
  80.9 22.7 %copy-start.8 = (f32[4096]{0:T(1024)S(1)}, f32[4096]{0:T(1024)}, u32[]{:S(2)}) copy-start(f32[4096]{0:T(1024)} %gain_ref.1) | copy-start | bytes 49156
  103.6 1.6 copy-start.1
  107.0 16.2 %copy-start.6 = (s32[8192]{0:T(1024)S(1)}, s32[8192]{0:T(1024)}, u32[]{:S(2)}) copy-start(s32[8192]{0:T(1024)} %param.13) | copy-start | bytes 98308
  119.4 18.6 %all-to-all-start.7 = ((bf16[16,64,256]{2,1,0:T(8,128)(2,1)}), bf16[16,64,256]{2,1,0:T(8,128)(2,1)S(1)}, u32[]{:S(2)}, u32[]{:S(2)}) async-start(bf16[16,64,256]{2,1,0:T(8,128)(2,1)} %get-tuple-element.8), calls=%async_computation.7 | async-start | bytes 1048576 | tf_op jit(solution)/shard_map/all_to_all | solution.py:29
where the time goes:
time: 166 us; the launch traced here: 164 us
  blocking collectives  95 us (57%)
  waiting for transfers between devices  37.4 us (23%)
  starting transfers between devices  13.5 us (8%)
  Pallas kernels  11.7 us (7%)
  local copies, waits for them, and re-layouts  5.45 us (3%)
    all_to_all x7, blocking collectives, exchange(): return lax.all_to_all(parts, axis, split_axis=0, concat_axis=0, tiled=True)  95 us
    all_to_all x3, waiting for transfers between devices, exchange(): return lax.all_to_all(parts, axis, split_axis=0, concat_axis=0, tiled=True)  37.4 us
    all_to_all x3, starting transfers between devices, exchange(): return lax.all_to_all(parts, axis, split_axis=0, concat_axis=0, tiled=True)  13.5 us
    unnamed x20, local copies, waits for them, and re-layouts  5.06 us
    pallas_call x1, Pallas kernels, attend(): pl.pallas_call(functools.partial(attend_kernel, pair), grid=(q_blocks,),...  4.31 us
  transfers between devices with their start and end apart: 3, of which 3 were waited for; matrix products, arithmetic and copies ran while one was open for 0% of the time, Pallas kernels for 0%

commit v1 on v0

--- a/solution.py
+++ b/solution.py
@@ -78,7 +78,10 @@
         ],
         compiler_params=params(),
         name="merge_up",
-    )(patches, vision_gain, merge_up.T)
+    )(*[
+        pltpu.with_memory_space_constraint(v, pltpu.HBM)
+        for v in (patches, vision_gain, merge_up.T)
+    ])
 
 
 def shuffle_kernel(n_x, rows_ref, out_ref):
@@ -404,6 +407,7 @@
     seen = seen_from(route_count, rows)
 
     hidden = merge_up_rows(patches, vision_gain, merge_up, n_y)
+    hidden, owner, home, half = lax.optimization_barrier((hidden, owner, home, half))
     hidden = exchange(shuffle_rows(exchange(hidden, "ctx_0"), n_x), CTX[1:])
     partial_sums = merge_down_rows(
         owner, route_count, hidden.reshape(rows, -1), merge_down, n_y, n_x, tp, grp

time: 166 us -> 160 us (0.964)
  blocking collectives: 95 us -> 127 us
  waiting for transfers between devices: 37.4 us -> 14.3 us
  starting transfers between devices: 13.5 us -> 3.57 us
  local copies, waits for them, and re-layouts: 5.45 us -> 0.42 us
    all_to_all x7 -> x9, blocking collectives: 95 us -> 127 us  [exchange(): return lax.all_to_all(parts, axis, split_axis=0, concat_axis=0, tiled=True)]
    all_to_all x3 -> x1, waiting for transfers between devices: 37.4 us -> 14.3 us  [exchange(): return lax.all_to_all(parts, axis, split_axis=0, concat_axis=0, tiled=True)]
    all_to_all x3 -> x1, starting transfers between devices: 13.5 us -> 3.57 us  [exchange(): return lax.all_to_all(parts, axis, split_axis=0, concat_axis=0, tiled=True)]
    unnamed x20 -> x14, local copies, waits for them, and re-layouts: 5.06 us -> 0.03 us
  transfers between devices with their start and end apart: 3 -> 1, of which waited for: 3 -> 1; matrix products, arithmetic and copies ran while one was open for 0% -> 0% of each run, Pallas kernels for 0% -> 0%
where the time goes in v1:
time: 160 us; the launch traced here: 157 us
  blocking collectives  127 us (79%)
  waiting for transfers between devices  14.3 us (9%)
  Pallas kernels  11.5 us (7%)
  starting transfers between devices  3.57 us (2%)
    all_to_all x9, blocking collectives, exchange(): return lax.all_to_all(parts, axis, split_axis=0, concat_axis=0, tiled=True)  127 us
    all_to_all x1, waiting for transfers between devices, exchange(): return lax.all_to_all(parts, axis, split_axis=0, concat_axis=0, tiled=True)  14.3 us
    pallas_call x1, Pallas kernels, attend(): pl.pallas_call(functools.partial(attend_kernel, pair), grid=(q_blocks,),...  4.31 us
    all_to_all x1, starting transfers between devices, exchange(): return lax.all_to_all(parts, axis, split_axis=0, concat_axis=0, tiled=True)  3.57 us
    pallas_call x1, Pallas kernels, merge_up_rows(): pl.pallas_call(up_kernel, in_specs=[pl.BlockSpec(memory_space=pltpu.HBM)]...  3.24 us
  transfers between devices with their start and end apart: 1, of which 1 were waited for; matrix products, arithmetic and copies ran while one was open for 0% of the time, Pallas kernels for 0%

profile of v1, /device:TPU:1, one launch (start us, length us, event | category | flops | bytes accessed | tf_op | source)
XLA Modules:
  0.0 157.5 jit_solution(2001558489613087057)
XLA Ops:
  0.0 3.2 %merge_up.1 = bf16[8,16,160]{2,1,0:T(8,128)(2,1)S(1)} custom-call(bf16[128,5120]{1,0:T(8,128)(2,1)} %x_hbm.1, f32[1280]{0:T(1024)} %gain_hbm.1, bf16[160,5120]{1,0:T(8,128)(2,1)} %bitcast.29), custom_call_target="tpu_custom_call" | custom-call | tf_op jit(solution)/shard_map/merge_up/pallas_call | solution.py:67
  3.3 0.1 pad_add_fusion.1.home_ref
  3.3 15.1 %all_to_all.50.rows_ref = bf16[8,16,160]{2,1,0:T(8,128)(2,1)S(1)} all-to-all(bf16[8,16,160]{2,1,0:T(8,128)(2,1)S(1)} %merge_up.1), channel_id=1, replica_groups=mesh['ctx_0'=8,'ctx_q'=4,'ctx_p'=2,'tp'=8,'grp'=2] {'ctx_0'}, dimensions={0} | all-to-all | bytes 81920 | tf_op jit(solution)/shard_map/all_to_all | solution.py:29
  18.4 0.1 shuffle.1
  18.6 13.6 %all_to_all.51 = bf16[8,16,160]{2,1,0:T(8,128)(2,1)S(1)} all-to-all(bf16[8,16,160]{2,1,0:T(8,128)(2,1)S(1)} %shuffle.1), channel_id=1, replica_groups=mesh['ctx_0'=8,'ctx_q'=4,'ctx_p'=2,'tp'=8,'grp'=2] {'ctx_q','ctx_p'}, dimensions={0} | all-to-all | bytes 81920 | tf_op jit(solution)/shard_map/all_to_all | solution.py:29
  32.2 0.0 copy-done.2
  32.2 0.0 copy-done.3
  32.2 0.6 merge_down.1
  32.8 11.1 %all_to_all.52.parts_ref = bf16[2,8,128,256]{3,2,1,0:T(8,128)(2,1)S(1)} all-to-all(bf16[2,8,128,256]{3,2,1,0:T(8,128)(2,1)S(1)} %merge_down.1), channel_id=1, replica_groups=mesh['ctx_0'=8,'ctx_q'=4,'ctx_p'=2,'tp'=8,'grp'=2] {'grp'}, dimensions={0} | all-to-all | bytes 2097152 | tf_op jit(solution)/shard_map/all_to_all | solution.py:29
  43.9 0.1 pair_sum.1
  44.1 29.5 %all_to_all.53.parts_ref = bf16[8,128,256]{2,1,0:T(8,128)(2,1)S(1)} all-to-all(bf16[8,128,256]{2,1,0:T(8,128)(2,1)S(1)} %pair_sum.1), channel_id=1, replica_groups=mesh['ctx_0'=8,'ctx_q'=4,'ctx_p'=2,'tp'=8,'grp'=2] {'tp'}, dimensions={0} | all-to-all | bytes 1048576 | tf_op jit(solution)/shard_map/all_to_all | solution.py:29
  73.5 0.0 copy-done.5
  73.5 0.2 place.1
  73.7 0.0 copy-start.1
  73.7 17.7 %all_to_all.54 = bf16[8,128,256]{2,1,0:T(8,128)(2,1)S(1)} all-to-all(bf16[8,128,256]{2,1,0:T(8,128)(2,1)S(1)} %place.1), channel_id=1, replica_groups=mesh['ctx_0'=8,'ctx_q'=4,'ctx_p'=2,'tp'=8,'grp'=2] {'tp'}, dimensions={0} | all-to-all | bytes 1048576 | tf_op jit(solution)/shard_map/all_to_all | solution.py:29
  91.4 0.1 broadcast_in_dim.4
  91.5 7.7 %all_to_all.55.parts_ref = bf16[2,8,128,256]{3,2,1,0:T(8,128)(2,1)S(1)} all-to-all(bf16[2,8,128,256]{3,2,1,0:T(8,128)(2,1)S(1)} %broadcast_in_dim.4), channel_id=1, replica_groups=mesh['ctx_0'=8,'ctx_q'=4,'ctx_p'=2,'tp'=8,'grp'=2] {'grp'}, dimensions={0} | all-to-all | bytes 2097152 | tf_op jit(solution)/shard_map/all_to_all | solution.py:29
  99.1 0.0 copy-done.1
  99.1 0.0 copy-done
  99.1 0.0 copy-done.6
  99.2 1.8 %project.1 = (bf16[4,128,256]{2,1,0:T(8,128)(2,1)S(1)}, bf16[16,64,256]{2,1,0:T(8,128)(2,1)}) custom-call(s32[1]{0:T(128)} %bitcast.5.half_ref, bf16[2,8,128,256]{3,2,1,0:T(8,128)(2,1)S(1)} %all_to_all.55.parts_ref, f32[4096]{0:T(1024)S(1)} %copy-done.6, bf16[4096,256]{1,0:T(8,128)(2,1)S(1)} %copy-done, bf16[4096,256]{1,0:T(8,128)(2,1)S(1)} %copy-done.1), custom_call_target="tpu_custom_call" | custom-call | tf_op jit(solution)/shard_map/project/pallas_call | solution.py:220
  101.0 12.3 %all_to_all.56.q_ref = bf16[4,128,256]{2,1,0:T(8,128)(2,1)S(1)} all-to-all(bf16[4,128,256]{2,1,0:T(8,128)(2,1)S(1)} %get-tuple-element.15), channel_id=1, replica_groups=mesh['ctx_0'=8,'ctx_q'=4,'ctx_p'=2,'tp'=8,'grp'=2] {'ctx_q'}, dimensions={0} | all-to-all | bytes 524288 | tf_op jit(solution)/shard_map/all_to_all | solution.py:29
  113.3 3.6 %all-to-all-start.7 = ((bf16[16,64,256]{2,1,0:T(8,128)(2,1)}), bf16[16,64,256]{2,1,0:T(8,128)(2,1)S(1)}, u32[]{:S(2)}, u32[]{:S(2)}) async-start(bf16[16,64,256]{2,1,0:T(8,128)(2,1)} %get-tuple-element.16), calls=%async_computation.7 | async-start | bytes 1048576 | tf_op jit(solution)/shard_map/all_to_all | solution.py:29
  116.9 0.2 seen.1.seen_ref
  117.1 0.2 slice_reduce_fusion.1
  117.3 0.3 convert_reduce_fusion.1
  117.6 14.3 %all-to-all-done.7 = bf16[16,64,256]{2,1,0:T(8,128)(2,1)S(1)} async-done(((bf16[16,64,256]{2,1,0:T(8,128)(2,1)}), bf16[16,64,256]{2,1,0:T(8,128)(2,1)S(1)}, u32[]{:S(2)}, u32[]{:S(2)}) %all-to-all-start.7) | async-done | bytes 524320 | tf_op jit(solution)/shard_map/all_to_all | solution.py:29
  131.9 0.1 broadcast_in_dim.5
  132.0 7.1 %all_to_all.57.kv_ref = bf16[2,16,64,256]{3,2,1,0:T(8,128)(2,1)S(1)} all-to-all(bf16[2,16,64,256]{3,2,1,0:T(8,128)(2,1)S(1)} %broadcast_in_dim.5), channel_id=1, replica_groups=mesh['ctx_0'=8,'ctx_q'=4,'ctx_p'=2,'tp'=8,'grp'=2] {'grp'}, dimensions={0} | all-to-all | bytes 2097152 | tf_op jit(solution)/shard_map/all_to_all | solution.py:29
  139.1 4.3 %attend.1 = bf16[4,144,256]{2,1,0:T(8,128)(2,1)S(1)} custom-call(s32[3]{0:T(128)S(1)} %pad_add_fusion.1.home_ref, s32[2,4]{1,0:T(2,128)S(1)} %pad_add_fusion.ends_ref, bf16[4,128,256]{2,1,0:T(8,128)(2,1)S(1)} %all_to_all.56.q_ref, bf16[2,16,64,256]{3,2,1,0:T(8,128)(2,1)S(1)} %all_to_all.57.kv_ref, s32[64,128]{1,0:T(8,128)S(1)} %bitcast.28, ...), custom_call_target="tpu_custom_call" | custom-call | tf_op jit(solution)/shard_map/attend/pallas_call | solution.py:326
  143.5 13.1 %all_to_all.58.parts_ref = bf16[4,144,256]{2,1,0:T(8,128)(2,1)S(1)} all-to-all(bf16[4,144,256]{2,1,0:T(8,128)(2,1)S(1)} %attend.1), channel_id=1, replica_groups=mesh['ctx_0'=8,'ctx_q'=4,'ctx_p'=2,'tp'=8,'grp'=2] {'ctx_q'}, dimensions={0} | all-to-all | bytes 589824 | tf_op jit(solution)/shard_map/all_to_all | solution.py:29
  156.6 0.9 combine.1
  (10 shorter events, 0.0 us)
Async XLA Ops:
  0.0 32.2 %copy-start.2 = (bf16[160,4096]{1,0:T(8,128)(2,1)S(1)}, bf16[160,4096]{1,0:T(8,128)(2,1)}, u32[]{:S(2)}) copy-start(bf16[160,4096]{1,0:T(8,128)(2,1)} %w_ref.1) | copy-start | bytes 3932164
  0.0 32.2 %copy-start.3 = (s32[64,64]{1,0:T(8,128)S(1)}, s32[64,64]{1,0:T(8,128)}, u32[]{:S(2)}) copy-start(s32[64,64]{1,0:T(8,128)} %route_ref.5) | copy-start | bytes 49156
  43.9 29.6 %copy-start.5 = (bf16[128,256]{1,0:T(8,128)(2,1)S(1)}, bf16[128,256]{1,0:T(8,128)(2,1)}, u32[]{:S(2)}) copy-start(bf16[128,256]{1,0:T(8,128)(2,1)} %text_ref.1) | copy-start | bytes 196612
  73.7 25.4 %copy-start.1 = (bf16[4096,256]{1,0:T(8,128)(2,1)S(1)}, bf16[4096,256]{1,0:T(8,128)(2,1)}, u32[]{:S(2)}) copy-start(bf16[4096,256]{1,0:T(8,128)(2,1)} %wkv_ref.1) | copy-start | bytes 6291460
  91.4 7.8 %copy-start = (bf16[4096,256]{1,0:T(8,128)(2,1)S(1)}, bf16[4096,256]{1,0:T(8,128)(2,1)}, u32[]{:S(2)}) copy-start(bf16[4096,256]{1,0:T(8,128)(2,1)} %wq_ref.1) | copy-start | bytes 6291460
  91.4 7.8 %copy-start.6 = (f32[4096]{0:T(1024)S(1)}, f32[4096]{0:T(1024)}, u32[]{:S(2)}) copy-start(f32[4096]{0:T(1024)} %gain_ref.1) | copy-start | bytes 49156
  101.0 16.1 %copy-start.4 = (s32[8192]{0:T(1024)S(1)}, s32[8192]{0:T(1024)}, u32[]{:S(2)}) copy-start(s32[8192]{0:T(1024)} %param.13) | copy-start | bytes 98308
  113.3 18.6 %all-to-all-start.7 = ((bf16[16,64,256]{2,1,0:T(8,128)(2,1)}), bf16[16,64,256]{2,1,0:T(8,128)(2,1)S(1)}, u32[]{:S(2)}, u32[]{:S(2)}) async-start(bf16[16,64,256]{2,1,0:T(8,128)(2,1)} %get-tuple-element.16), calls=%async_computation.7 | async-start | bytes 1048576 | tf_op jit(solution)/shard_map/all_to_all | solution.py:29
